TPU v7x, 512 devices: a 4x2x32 block of a 4x8x32 slice. The times are simulated.
512 devices in a mesh: grp: 2 (over y), blk: 128 (over z, x), uly: 2 (over core).
Axes of the slice: x: 4, y: 2, z: 32, core: 2. Of those that a mesh axis runs over, the one named last changes fastest.
The devices are a block of a 4x8x32 slice.
Arguments:
- query: bfloat16 [8192, 1152], P(('grp', 'blk', 'uly')), parts along dimension 0, may hold values from -6 to 6
- key: bfloat16 [8192, 1152], P(('grp', 'blk', 'uly')), parts along dimension 0, may hold values from -6 to 6
- value: bfloat16 [8192, 1152], P(('grp', 'blk', 'uly')), parts along dimension 0, may hold values from -6 to 6
- q_gain: float32 [96], replicated, may hold values from 1 to 2.5
- k_gain: float32 [96], replicated, may hold values from 1 to 2.5
- out_weight: bfloat16 [1152, 2304], P('uly'), may hold values from -0.1875 to 0.1875
Outputs:
- mixed: bfloat16 [8192, 2304], P(('grp', 'blk', 'uly')), parts along dimension 0
There are 2 independent parts, one for each index of `grp`. A program takes and returns all parts, laid end to end along the dimension named above; an argument that names none is the same for every part. Nothing has to cross between parts.
All inputs are finite; a program needn't handle non-finite values.
Results may differ from a plain program's by a relative error of at most 0.012.
Values may be sent and summed in bfloat16 or wider, within the bound.
A program may use at most 128 MiB of HBM per device.

v0:
```python
import jax
import jax.numpy as jnp
from jax import lax
from jax.sharding import Mesh
from jax.sharding import PartitionSpec as P

H = 12
HD = 96
GRP_BLK_ULY = ("grp", "blk_0", "blk_1", "uly")


def whole_of(shard, axes, dim):
    if not axes:
        return shard
    nearer = lax.all_gather(shard, axes[-1], axis=dim, tiled=True)
    return whole_of(nearer, axes[:-1], dim)


def split_up(shard, dim, length):
    dims = shard.shape
    blocks = shard.reshape(*dims[:dim], length, dims[dim] // length, *dims[dim + 1 :])
    return jnp.moveaxis(blocks, dim, 0)


def sent_and_summed(shard, axis, dim):
    length = lax.axis_size(axis)
    blocks = lax.all_to_all(split_up(shard, dim, length), axis, 0, 0, tiled=True)
    return jnp.sum(blocks.astype(jnp.float32), axis=0)


def normed(data, gain):
    tok_rows = data.shape[0]
    grid = data.astype(jnp.float32).reshape(tok_rows, H, HD)
    meansq = jnp.mean(grid * grid, axis=-1, keepdims=True)
    return (grid * lax.rsqrt(meansq + 1e-06) * gain).astype(jnp.bfloat16).reshape(tok_rows, H * HD)


def attend_block(query_heads, kv_piece):
    length = kv_piece.shape[1]
    head_count = query_heads.shape[1]
    key_heads = kv_piece[0].reshape(length, head_count, HD)
    value_heads = kv_piece[1].reshape(length, head_count, HD)
    score_scale = float(HD) ** (-0.5)
    scores = (
        jnp.einsum("qhd,khd->hqk", query_heads, key_heads, preferred_element_type=jnp.float32)
        * score_scale
    )
    expd = jnp.exp(scores)
    total_weight = jnp.sum(expd, axis=-1).T
    weighted = jnp.einsum(
        "hqk,khd->qhd", expd.astype(jnp.bfloat16), value_heads, preferred_element_type=jnp.float32
    )
    return (weighted, total_weight)


def on_device(query, key, value, q_gain, k_gain, out_weight):
    query_normed = normed(query, q_gain)
    key_normed = normed(key, k_gain)
    query_group, key_group, value_group = (
        lax.all_to_all(query_normed, "uly", split_axis=1, concat_axis=0, tiled=True),
        lax.all_to_all(key_normed, "uly", split_axis=1, concat_axis=0, tiled=True),
        lax.all_to_all(value, "uly", split_axis=1, concat_axis=0, tiled=True),
    )
    row_count = query_group.shape[0]
    local_heads = query_group.shape[1] // HD
    query_heads = query_group.reshape(row_count, local_heads, HD)
    kv_stack = jnp.stack([key_group, value_group])
    weighted, total_weight = attend_block(query_heads, whole_of(kv_stack, ("blk_1", "blk_0"), 1))
    attn = (
        (weighted / total_weight[:, :, None])
        .astype(jnp.bfloat16)
        .reshape(row_count, local_heads * HD)
    )
    mixed = sent_and_summed(
        jnp.dot(attn, out_weight, preferred_element_type=jnp.float32).astype(jnp.bfloat16), "uly", 0
    )
    return mixed.astype(jnp.bfloat16)


def solution(mesh):
    split = Mesh(
        mesh.devices.reshape(mesh.shape["grp"], 32, 4, mesh.shape["uly"]),
        ("grp", "blk_0", "blk_1", "uly"),
    )
    in_specs = (
        P(GRP_BLK_ULY, None),
        P(GRP_BLK_ULY, None),
        P(GRP_BLK_ULY, None),
        P(),
        P(),
        P("uly", None),
    )
    out_specs = P(GRP_BLK_ULY, None)
    return jax.shard_map(
        on_device, mesh=split, in_specs=in_specs, out_specs=out_specs, check_vma=False
    )
```

profile of v0, /device:TPU:33, one launch (start us, length us, event | category | flops | bytes accessed | tf_op | source)
XLA Modules:
  0.0 334.8 jit_solution(16086594618422082272)
XLA Ops:
  6.6 0.9 convert_multiply_fusion.3
  7.9 0.7 mul.71
  8.7 0.8 fusion.13
  9.5 0.1 all_to_all.39
  9.6 0.6 copy.22
  10.2 44.7 %all-to-all-start = ((bf16[16,2,576]{2,0,1:T(8,128)(2,1)}), bf16[16,2,576]{2,0,1:T(8,128)(2,1)S(1)}, u32[]{:S(2)}, u32[]{:S(2)}) async-start(bf16[16,2,576]{2,0,1:T(8,128)(2,1)} %copy.22), calls=%async_computation | async-start | bytes 81920 | tf_op jit(solution)/shard_map/all_to_all | solution.py:61
  54.9 0.9 all_to_all.42
  55.8 0.2 all-to-all-done
  56.0 3.8 %all_to_all.53 = bf16[16,2,576]{2,0,1:T(8,128)(2,1)S(1)} all-to-all(bf16[16,2,576]{2,0,1:T(8,128)(2,1)S(1)} %copy.23), channel_id=1, replica_groups=mesh['grp'=2,'blk_0'=32,'blk_1'=4,'uly'=2] {'uly'}, dimensions={1} | all-to-all | bytes 73728 | tf_op jit(solution)/shard_map/all_to_all | solution.py:62
  59.7 0.6 pad_maximum_fusion
  60.5 101.1 %all-gather.3.cloned.1.call-done = bf16[2,1024,576]{2,1,0:T(8,128)(2,1)} async-done(((bf16[2,32,576]{2,1,0:T(8,128)(2,1)}), bf16[2,1024,576]{2,1,0:T(8,128)(2,1)}) %all-gather.3.cloned.1.call-update) | async-done | bytes 2359312 | tf_op jit(solution)/shard_map/all_gather | solution.py:15
  161.7 0.8 convert_multiply_fusion.1
  163.1 25.3 %all_to_all.54 = bf16[16,2,576]{2,0,1:T(8,128)(2,1)S(1)} all-to-all(bf16[16,2,576]{2,0,1:T(8,128)(2,1)S(1)} %copy.25), channel_id=1, replica_groups=mesh['grp'=2,'blk_0'=32,'blk_1'=4,'uly'=2] {'uly'}, dimensions={1} | all-to-all | bytes 73728 | tf_op jit(solution)/shard_map/all_to_all | solution.py:60
  188.5 0.1 reshape.50
  188.6 104.1 %all-gather.5.cloned.1.call-done = bf16[2,4096,576]{2,1,0:T(8,128)(2,1)} async-done(((bf16[2,1024,576]{2,1,0:T(8,128)(2,1)}), bf16[2,4096,576]{2,1,0:T(8,128)(2,1)}) %all-gather.5.cloned.1.call-update) | async-done | bytes 9437200 | tf_op jit(solution)/shard_map/all_gather | solution.py:15
  292.6 8.9 %fusion.17 = (bf16[1,4096,576]{2,1,0:T(8,128)(2,1)}, bf16[1,4096,576]{2,1,0:T(8,128)(2,1)}) fusion(bf16[2,4096,576]{2,1,0:T(8,128)(2,1)} %all-gather.5.cloned.1.call-done), kind=kLoop, calls=%fused_computation.20 | loop fusion | bytes 18874368 | tf_op jit(solution)/shard_map/slice | solution.py:41
  301.5 7.6 %copy.26 = bf16[1,4096,576]{1,2,0:T(8,128)(2,1)} copy(bf16[1,4096,576]{2,1,0:T(8,128)(2,1)} %get-tuple-element.5) | data formatting | bytes 9437184 | tf_op jit(solution)/shard_map/slice | solution.py:41
  309.2 7.6 %copy.24 = bf16[1,4096,576]{1,2,0:T(8,128)(2,1)} copy(bf16[1,4096,576]{2,1,0:T(8,128)(2,1)} %get-tuple-element.6) | data formatting | bytes 9437184 | tf_op jit(solution)/shard_map/slice | solution.py:42
  316.8 3.5 %fusion.18 = (f32[6,32]{1,0:T(8,128)S(1)}, bf16[6,32,4096]{2,1,0:T(8,128)(2,1)S(1)}) fusion(bf16[4096,6,96]{0,2,1:T(8,128)(2,1)} %bitcast.22, bf16[32,6,96]{2,1,0:T(8,128)(2,1)S(1)} %reshape.50), kind=kOutput, calls=%fused_computation.21 | convolution fusion | flops 153354048 | bytes 6329088 | tf_op jit(solution)/shard_map/qhd,khd->hqk/dot_general | solution.py:45
  320.3 0.3 copy-done.1
  320.5 1.8 fusion.9
  322.5 0.5 convolution_convert_fusion
  323.0 4.3 %all_to_all.55 = bf16[2,16,2304]{2,1,0:T(8,128)(2,1)S(1)} all-to-all(bf16[2,16,2304]{2,1,0:T(8,128)(2,1)S(1)} %bitcast.24), channel_id=1, replica_groups=mesh['grp'=2,'blk_0'=32,'blk_1'=4,'uly'=2] {'uly'}, dimensions={0} | all-to-all | bytes 294912 | tf_op jit(solution)/shard_map/all_to_all | solution.py:27
  327.3 0.7 reduce_sum.42
  (30 shorter events, 1.4 us)
Async XLA Ops:
  6.5 315.9 %copy-start = (bf16[576,2304]{1,0:T(8,128)(2,1)S(1)}, bf16[576,2304]{1,0:T(8,128)(2,1)}, u32[]{:S(2)}) copy-start(bf16[576,2304]{1,0:T(8,128)(2,1)} %param.11) | copy-start | bytes 7962628
  6.6 156.4 %copy-start.2 = (bf16[16,1152]{1,0:T(8,128)(2,1)S(1)}, bf16[16,1152]{1,0:T(8,128)(2,1)}, u32[]{:S(2)}) copy-start(bf16[16,1152]{1,0:T(8,128)(2,1)} %param.6) | copy-start | bytes 110596
  6.6 156.3 %copy-start.3 = (f32[96]{0:T(128)S(1)}, f32[96]{0:T(128)}, u32[]{:S(2)}) copy-start(f32[96]{0:T(128)} %param.9) | copy-start | bytes 1156
  10.2 45.8 %all-to-all-start = ((bf16[16,2,576]{2,0,1:T(8,128)(2,1)}), bf16[16,2,576]{2,0,1:T(8,128)(2,1)S(1)}, u32[]{:S(2)}, u32[]{:S(2)}) async-start(bf16[16,2,576]{2,0,1:T(8,128)(2,1)} %copy.22), calls=%async_computation | async-start | bytes 81920 | tf_op jit(solution)/shard_map/all_to_all | solution.py:61
  54.9 106.7 %all-gather.3.cloned.1.call-start = ((), (), s32[]{:S(2)}) async-start(), calls=%async_computation.4 | async-start | bytes 2703360 | tf_op jit(solution)/shard_map/all_gather | solution.py:15
  60.4 232.2 %all-gather.5.cloned.1.call-start = ((), (), s32[]{:S(2)}) async-start(), calls=%async_computation.5 | async-start | bytes 13107200 | tf_op jit(solution)/shard_map/all_gather | solution.py:15
  316.8 3.8 %copy-start.1 = (bf16[1,4096,576]{1,2,0:T(8,128)(2,1)S(1)}, bf16[1,4096,576]{1,2,0:T(8,128)(2,1)}, u32[]{:S(2)}) copy-start(bf16[1,4096,576]{1,2,0:T(8,128)(2,1)} %copy.24) | copy-start | bytes 14155780
Sparse Core Ops, SparseCore 0:
  60.5 101.0 all-gather.2
  163.7 128.8 all-gather.4
where the time goes:
time: 336 us; the launch traced here: 335 us
  waiting for transfers between devices  205 us (61%)
  starting transfers between devices  44.8 us (13%)
  blocking collectives  33.4 us (10%)
  local copies, waits for them, and re-layouts  27.8 us (8%)
  between operations  13.6 us (4%)
  matrix products  5.82 us (2%)
  other arithmetic  4.04 us (1%)
    all_gather x2, waiting for transfers between devices, whole_of(): nearer = lax.all_gather(shard, axes[-1], axis=dim, tiled=True)  205 us
    all_to_all x1, starting transfers between devices, on_device(): lax.all_to_all(key_normed, 'uly', split_axis=1, concat_axis=0, tiled=True)  44.7 us
    all_to_all x1, blocking collectives, on_device(): lax.all_to_all(query_normed, 'uly', split_axis=1, concat_axis=0, tiled=True)  25.3 us
    slice x2, local copies, waits for them, and re-layouts, attend_block(): key_heads = kv_piece[0].reshape(length, head_count, HD)  16.5 us
    slice x1, local copies, waits for them, and re-layouts, attend_block(): value_heads = kv_piece[1].reshape(length, head_count, HD)  7.59 us
  transfers between devices with their start and end apart: 3, of which 3 were waited for; matrix products, arithmetic and copies ran while one was open for 0% of the time, Pallas kernels for 0%

commit v1 on v0

--- a/solution.py
+++ b/solution.py
@@ -3,10 +3,14 @@
 from jax import lax
 from jax.sharding import Mesh
 from jax.sharding import PartitionSpec as P
+from jax.lax import all_to_all, axis_size
 
 H = 12
 HD = 96
 GRP_BLK_ULY = ("grp", "blk_0", "blk_1", "uly")
+bind_cells = lambda arr_in, row_axis: jnp.concatenate(
+    all_to_all(jnp.stack(jnp.split(arr_in, axis_size(row_axis), 1)), row_axis, 0, 0), axis=0
+)
 
 
 def whole_of(shard, axes, dim):
@@ -57,7 +61,7 @@
     query_normed = normed(query, q_gain)
     key_normed = normed(key, k_gain)
     query_group, key_group, value_group = (
-        lax.all_to_all(query_normed, "uly", split_axis=1, concat_axis=0, tiled=True),
+        bind_cells(query_normed, "uly"),
         lax.all_to_all(key_normed, "uly", split_axis=1, concat_axis=0, tiled=True),
         lax.all_to_all(value, "uly", split_axis=1, concat_axis=0, tiled=True),
     )

time: 336 us -> 335 us (level)
  transfers between devices with their start and end apart: 3 -> 3, of which waited for: 3 -> 2; matrix products, arithmetic and copies ran while one was open for 0% -> 1% of each run, Pallas kernels for 0% -> 0%
where the time goes in v1:
time: 335 us; the launch traced here: 334 us
  waiting for transfers between devices  205 us (61%)
  starting transfers between devices  44.8 us (13%)
  blocking collectives  33.2 us (10%)
  local copies, waits for them, and re-layouts  27.7 us (8%)
  between operations  13.6 us (4%)
  matrix products  5.82 us (2%)
  other arithmetic  3.89 us (1%)
    all_gather x2, waiting for transfers between devices, whole_of(): nearer = lax.all_gather(shard, axes[-1], axis=dim, tiled=True)  205 us
    all_to_all x1, starting transfers between devices, on_device(): lax.all_to_all(value, 'uly', split_axis=1, concat_axis=0, tiled=True)  44.7 us
    all_to_all x1, blocking collectives, all_to_all(jnp.stack(jnp.split(arr_in, axis_size(row_axis), 1)), row_axis...  25.3 us
    slice x2, local copies, waits for them, and re-layouts, attend_block(): key_heads = kv_piece[0].reshape(length, head_count, HD)  16.4 us
    slice x1, local copies, waits for them, and re-layouts, attend_block(): value_heads = kv_piece[1].reshape(length, head_count, HD)  7.66 us
  transfers between devices with their start and end apart: 3, of which 2 were waited for; matrix products, arithmetic and copies ran while one was open for 1% of the time, Pallas kernels for 0%

profile of v1, /device:TPU:33, one launch (start us, length us, event | category | flops | bytes accessed | tf_op | source)
XLA Modules:
  0.0 334.3 jit_solution(15244721206752113820)
XLA Ops:
  6.6 1.0 all_to_all.33
  7.6 0.6 copy.21
  8.2 44.7 %all-to-all-start.1 = ((bf16[16,2,576]{2,0,1:T(8,128)(2,1)}), bf16[16,2,576]{2,0,1:T(8,128)(2,1)S(1)}, u32[]{:S(2)}, u32[]{:S(2)}) async-start(bf16[16,2,576]{2,0,1:T(8,128)(2,1)} %copy.21), calls=%async_computation.1 | async-start | bytes 81920 | tf_op jit(solution)/shard_map/all_to_all | solution.py:66
  52.9 0.8 convert_multiply_fusion.3
  54.1 0.7 mul.71
  54.9 0.8 fusion.13
  55.7 0.1 all_to_all.30
  55.8 3.5 %all_to_all.42 = bf16[16,2,576]{2,0,1:T(8,128)(2,1)S(1)} all-to-all(bf16[16,2,576]{2,0,1:T(8,128)(2,1)S(1)} %copy.20), channel_id=1, replica_groups=mesh['grp'=2,'blk_0'=32,'blk_1'=4,'uly'=2] {'uly'}, dimensions={1} | all-to-all | bytes 73728 | tf_op jit(solution)/shard_map/all_to_all | solution.py:65
  59.3 0.6 pad_maximum_fusion
  60.1 101.1 %all-gather.3.cloned.1.call-done = bf16[2,1024,576]{2,1,0:T(8,128)(2,1)} async-done(((bf16[2,32,576]{2,1,0:T(8,128)(2,1)}), bf16[2,1024,576]{2,1,0:T(8,128)(2,1)}) %all-gather.3.cloned.1.call-update) | async-done | bytes 2359312 | tf_op jit(solution)/shard_map/all_gather | solution.py:19
  161.3 0.8 convert_multiply_fusion.1
  162.1 0.1 mul.76
  162.7 25.3 %all_to_all.43 = bf16[2,16,576]{2,1,0:T(8,128)(2,1)S(1)} all-to-all(bf16[2,16,576]{2,1,0:T(8,128)(2,1)S(1)} %pad_maximum_fusion.1), channel_id=1, replica_groups=mesh['grp'=2,'blk_0'=32,'blk_1'=4,'uly'=2] {'uly'}, dimensions={0} | all-to-all | bytes 73728 | tf_op jit(solution)/shard_map/all_to_all | solution.py:12
  188.1 0.1 reshape_reshape.3
  188.2 104.1 %all-gather.5.cloned.1.call-done = bf16[2,4096,576]{2,1,0:T(8,128)(2,1)} async-done(((bf16[2,1024,576]{2,1,0:T(8,128)(2,1)}), bf16[2,4096,576]{2,1,0:T(8,128)(2,1)}) %all-gather.5.cloned.1.call-update) | async-done | bytes 9437200 | tf_op jit(solution)/shard_map/all_gather | solution.py:19
  292.3 8.8 %fusion.17 = (bf16[1,4096,576]{2,1,0:T(8,128)(2,1)}, bf16[1,4096,576]{2,1,0:T(8,128)(2,1)}) fusion(bf16[2,4096,576]{2,1,0:T(8,128)(2,1)} %all-gather.5.cloned.1.call-done), kind=kLoop, calls=%fused_computation.23 | loop fusion | bytes 18874368 | tf_op jit(solution)/shard_map/slice | solution.py:45
  301.0 7.7 %copy.22 = bf16[1,4096,576]{1,2,0:T(8,128)(2,1)} copy(bf16[1,4096,576]{2,1,0:T(8,128)(2,1)} %get-tuple-element.6) | data formatting | bytes 9437184 | tf_op jit(solution)/shard_map/slice | solution.py:46
  308.7 7.7 %copy.23 = bf16[1,4096,576]{1,2,0:T(8,128)(2,1)} copy(bf16[1,4096,576]{2,1,0:T(8,128)(2,1)} %get-tuple-element.5) | data formatting | bytes 9437184 | tf_op jit(solution)/shard_map/slice | solution.py:45
  316.4 3.5 %fusion.18 = (f32[6,32]{1,0:T(8,128)S(1)}, bf16[6,32,4096]{2,1,0:T(8,128)(2,1)S(1)}) fusion(bf16[4096,6,96]{0,2,1:T(8,128)(2,1)} %bitcast.25, bf16[32,6,96]{2,1,0:T(8,128)(2,1)S(1)} %reshape_reshape.3), kind=kOutput, calls=%fused_computation.24 | convolution fusion | flops 153354048 | bytes 6329088 | tf_op jit(solution)/shard_map/qhd,khd->hqk/dot_general | solution.py:49
  319.9 0.1 slice-done.1
  320.0 1.8 fusion.9
  321.9 0.5 convolution_convert_fusion
  322.5 4.3 %all_to_all.44 = bf16[2,16,2304]{2,1,0:T(8,128)(2,1)S(1)} all-to-all(bf16[2,16,2304]{2,1,0:T(8,128)(2,1)S(1)} %bitcast.29), channel_id=1, replica_groups=mesh['grp'=2,'blk_0'=32,'blk_1'=4,'uly'=2] {'uly'}, dimensions={0} | all-to-all | bytes 294912 | tf_op jit(solution)/shard_map/all_to_all | solution.py:31
  326.8 0.7 reduce_sum.42
  (33 shorter events, 1.3 us)
Async XLA Ops:
  6.5 315.4 %copy-start = (bf16[576,2304]{1,0:T(8,128)(2,1)S(1)}, bf16[576,2304]{1,0:T(8,128)(2,1)}, u32[]{:S(2)}) copy-start(bf16[576,2304]{1,0:T(8,128)(2,1)} %param.11) | copy-start | bytes 7962628
  6.6 156.1 %copy-start.1 = (bf16[16,1152]{1,0:T(8,128)(2,1)S(1)}, bf16[16,1152]{1,0:T(8,128)(2,1)}, u32[]{:S(2)}) copy-start(bf16[16,1152]{1,0:T(8,128)(2,1)} %param.6) | copy-start | bytes 110596
  6.6 156.0 %copy-start.2 = (f32[96]{0:T(128)S(1)}, f32[96]{0:T(128)}, u32[]{:S(2)}) copy-start(f32[96]{0:T(128)} %param.9) | copy-start | bytes 1156
  8.2 47.6 %all-to-all-start.1 = ((bf16[16,2,576]{2,0,1:T(8,128)(2,1)}), bf16[16,2,576]{2,0,1:T(8,128)(2,1)S(1)}, u32[]{:S(2)}, u32[]{:S(2)}) async-start(bf16[16,2,576]{2,0,1:T(8,128)(2,1)} %copy.21), calls=%async_computation.1 | async-start | bytes 81920 | tf_op jit(solution)/shard_map/all_to_all | solution.py:66
  52.9 108.3 %all-gather.3.cloned.1.call-start = ((), (), s32[]{:S(2)}) async-start(), calls=%async_computation.4 | async-start | bytes 2703360 | tf_op jit(solution)/shard_map/all_gather | solution.py:19
  60.0 232.2 %all-gather.5.cloned.1.call-start = ((), (), s32[]{:S(2)}) async-start(), calls=%async_computation.5 | async-start | bytes 13107200 | tf_op jit(solution)/shard_map/all_gather | solution.py:19
  308.7 11.2 %slice-start = ((s8[4718592]{0:T(1024)(128)(4,1)}), s8[524288]{0:T(1024)(128)(4,1)S(1)}, s32[]{:S(2)}) async-start(s8[4718592]{0:T(1024)(128)(4,1)} %bitcast.26), calls=%async_computation.6 | async-start | bytes 1048576
  316.4 3.6 %slice-start.1 = ((s8[4718592]{0:T(1024)(128)(4,1)}), s8[4194304]{0:T(1024)(128)(4,1)S(1)}, s32[]{:S(2)}) async-start(s8[4718592]{0:T(1024)(128)(4,1)} %bitcast.26), calls=%async_computation.7 | async-start | bytes 8388608
Sparse Core Ops, SparseCore 0:
  60.2 101.0 all-gather.2
  163.4 128.8 all-gather.4
